TPU v7x, 128 devices: a whole 4x4x4 slice. The times are simulated.
128 devices in a mesh: grp: 8 (over x_hi, y), mem: 16 (over z, x_lo, core).
Axes of the slice: x: 4 (x_hi: 2, x_lo: 2; x = x_hi * 2 + x_lo), y: 4, z: 4, core: 2. Of those that a mesh axis runs over, the one named last changes fastest.
Arguments:
- params: float32 [8, 2048, 2048], P('grp', 'mem'), may hold values from -6 to 6
- estimate: float32 [8, 2048, 2048], P('grp', 'mem'), may hold values from -6 to 6
- mixed_sum: float32 [8, 2048, 2048], P('grp', 'mem'), may hold values from -6 to 6
- activations: bfloat16 [131072, 2048], P(('grp', 'mem')), may hold values from -24 to 24
- out_grads: bfloat16 [131072, 2048], P(('grp', 'mem')), may hold values from -6 to 6
- exponents: int32 [8, 32], P('grp', 'mem'), may hold values from 0 to 3
- edge_weight: float32 [8], replicated, may hold values from 0.1 to 0.45
Outputs:
- new_params: float32 [8, 2048, 2048], P('grp', 'mem')
- new_estimate: float32 [8, 2048, 2048], P('grp', 'mem')
- new_mixed: float32 [8, 2048, 2048], P('grp', 'mem')
All inputs are finite; a program needn't handle non-finite values.
Results may differ from a plain program's by a relative error of at most 0.01.
Values may be sent and summed in bfloat16 or wider, within the bound.
A program may use at most 128 MiB of HBM per device.

v0:
```python
import math

import jax
import jax.numpy as jnp
from jax import lax
from jax.sharding import PartitionSpec as P

step_size = 0.5
mixing_rate = 0.4


def cut_along(value, dim, size):
    dims = value.shape
    blocks = value.reshape(*dims[:dim], size, dims[dim] // size, *dims[dim + 1 :])
    return jnp.moveaxis(blocks, dim, 0)


def summed_on_arrival(value, axis, dim):
    size = lax.axis_size(axis)
    blocks = lax.all_to_all(cut_along(value, dim, size), axis, 0, 0, tiled=True)
    return jnp.sum(blocks.astype(jnp.float32), axis=0)


def shifted(value, axis, steps):
    count = lax.axis_size(axis)
    pairs = [(source, (source + steps) % count) for source in range(count)]
    return lax.ppermute(value, axis, pairs)


def on_device(params, estimate, mixed_sum, activations, out_grads, exponents, edge_weight):
    members = lax.axis_size("mem")
    groups = lax.axis_size("grp")
    shard_rows = params.shape[1]
    width = params.shape[2]
    local_rows = activations.shape[0]
    dims = (((0,), (0,)), ((), ()))
    gradient = summed_on_arrival(
        lax.dot_general(activations, out_grads, dims, preferred_element_type=jnp.float32).astype(
            jnp.bfloat16
        ),
        "mem",
        0,
    )
    factor = step_size / math.sqrt(members * local_rows)
    stepped = params - factor * gradient[None]
    change = stepped - estimate
    block_count = exponents.shape[1]
    scales = jnp.exp2(exponents.astype(jnp.float32))[:, :, None, None]
    blocked = change.reshape(1, block_count, shard_rows // block_count, width)
    levels = lax.optimization_barrier(jnp.clip(blocked / scales, -1.0, 1.0).astype(jnp.bfloat16))
    compressed = (
        (levels.astype(jnp.float32) * scales).astype(jnp.bfloat16).reshape(1, shard_rows, width)
    )
    left_piece = shifted(compressed, "grp", 1)
    right_piece = shifted(compressed, "grp", -1)
    own_piece = compressed.astype(jnp.float32)
    new_estimate = estimate + own_piece
    group_index = lax.axis_index("grp")
    weight_right = lax.dynamic_index_in_dim(edge_weight, group_index, 0, keepdims=False)
    weight_left = lax.dynamic_index_in_dim(
        edge_weight, (group_index + groups - 1) % groups, 0, keepdims=False
    )
    weight_self = 1.0 - weight_left - weight_right
    new_mixed = mixed_sum + weight_self * own_piece
    new_mixed = new_mixed + weight_left * left_piece.astype(jnp.float32)
    new_mixed = new_mixed + weight_right * right_piece.astype(jnp.float32)
    new_params = stepped + mixing_rate * (new_mixed - new_estimate)
    return (new_params, new_estimate, new_mixed)


def solution(mesh):
    in_specs = (
        P("grp", "mem", None),
        P("grp", "mem", None),
        P("grp", "mem", None),
        P(("grp", "mem"), None),
        P(("grp", "mem"), None),
        P("grp", "mem"),
        P(),
    )
    out_specs = (P("grp", "mem", None), P("grp", "mem", None), P("grp", "mem", None))
    return jax.shard_map(
        on_device, mesh=mesh, in_specs=in_specs, out_specs=out_specs, check_vma=False
    )
```

profile of v0, /device:TPU:0, one launch (start us, length us, event | category | flops | bytes accessed | tf_op | source)
XLA Modules:
  0.0 150.5 jit_solution(13377761376014496251)
XLA Ops:
  0.6 14.0 %convolution_convert_fusion = bf16[2048,2048]{1,0:T(8,128)(2,1)} fusion(bf16[1024,2048]{1,0:T(8,128)(2,1)} %param.10, bf16[1024,2048]{1,0:T(8,128)(2,1)} %param.11), kind=kOutput, calls=%fused_computation.1 | convolution fusion | flops 8594128896 | bytes 16777216 | tf_op jit(solution)/shard_map/dot_general | solution.py:38
  14.6 0.0 copy-start.3
  14.7 6.6 %all-to-all-start = ((bf16[16,128,2048]{2,1,0:T(8,128)(2,1)}), bf16[16,128,2048]{2,1,0:T(8,128)(2,1)}, u32[]{:S(2)}, u32[]{:S(2)}) async-start(bf16[16,128,2048]{2,1,0:T(8,128)(2,1)} %bitcast.19), calls=%async_computation | async-start | bytes 16777216 | tf_op jit(solution)/shard_map/all_to_all | solution.py:20
  21.3 0.0 copy-done.3
  21.3 0.0 copy-start
  21.3 0.0 copy-start.1
  21.3 95.2 %all-to-all-done = bf16[16,128,2048]{2,1,0:T(8,128)(2,1)} async-done(((bf16[16,128,2048]{2,1,0:T(8,128)(2,1)}), bf16[16,128,2048]{2,1,0:T(8,128)(2,1)}, u32[]{:S(2)}, u32[]{:S(2)}) %all-to-all-start) | async-done | bytes 8388640 | tf_op jit(solution)/shard_map/all_to_all | solution.py:20
  116.6 5.3 %convert_reduce_fusion = f32[128,2048]{1,0:T(8,128)S(1)} fusion(bf16[16,128,2048]{2,1,0:T(8,128)(2,1)} %all-to-all-done), kind=kLoop, calls=%fused_computation | loop fusion | flops 8126464 | bytes 9437184 | tf_op jit(solution)/shard_map/reduce_sum | solution.py:21
  121.9 0.0 copy-done
  121.9 0.0 copy-done.1
  121.9 0.0 copy-start.2
  121.9 0.2 fusion.3
  122.1 0.2 clamp_convert_fusion
  122.3 1.0 multiply_convert_fusion
  123.3 5.2 %collective-permute-start.1 = (bf16[1,128,2048]{2,1,0:T(8,128)(2,1)}, bf16[1,128,2048]{2,1,0:T(8,128)(2,1)}, u32[]{:S(2)}, u32[]{:S(2)}) collective-permute-start(bf16[1,128,2048]{2,1,0:T(8,128)(2,1)} %bitcast.6), channel_id=1, source_target_pairs={{0,112},{16,0},{32,16},{48,32},{64,48},{80,64},{96,80},{112,96},{1... | collective-permute-start | bytes 1572872 | tf_op jit(solution)/shard_map/ppermute | solution.py:27
  128.4 0.0 collective-permute-start
  128.4 0.0 copy-done.2
  128.4 0.6 fusion.5
  130.4 9.3 %collective-permute-done.1 = bf16[1,128,2048]{2,1,0:T(8,128)(2,1)} collective-permute-done((bf16[1,128,2048]{2,1,0:T(8,128)(2,1)}, bf16[1,128,2048]{2,1,0:T(8,128)(2,1)}, u32[]{:S(2)}, u32[]{:S(2)}) %collective-permute-start.1) | collective-permute-done | bytes 524320 | tf_op jit(solution)/shard_map/ppermute | solution.py:27
  139.6 5.8 %collective-permute-done = bf16[1,128,2048]{2,1,0:T(8,128)(2,1)} collective-permute-done((bf16[1,128,2048]{2,1,0:T(8,128)(2,1)}, bf16[1,128,2048]{2,1,0:T(8,128)(2,1)}, u32[]{:S(2)}, u32[]{:S(2)}) %collective-permute-start) | collective-permute-done | bytes 524320 | tf_op jit(solution)/shard_map/ppermute | solution.py:27
  145.5 5.1 %multiply_add_fusion = (f32[1,128,2048]{2,1,0:T(8,128)}, f32[1,128,2048]{2,1,0:T(8,128)}, f32[1,128,2048]{2,1,0:T(8,128)}) fusion(f32[1,128,2048]{2,1,0:T(8,128)S(1)} %copy-done, f32[128,2048]{1,0:T(8,128)S(1)} %convert_reduce_fusion, f32[1,128,2048]{2,1,0:T(8,128)S(1)} %copy-done.1, bf16[1,2,64,2048]{3,2,1,0:T(8,128)(2,1)} %multiply_convert_fusion, ...), kind=kLoop, calls=%fused_computation.8 | loop fusion | flops 3932160 | bytes 8912908 | tf_op jit(solution)/shard_map/add | solution.py:67
  (1 shorter events, 0.0 us)
Async XLA Ops:
  14.6 6.7 %copy-start.3 = (s32[1,2]{1,0:T(1,128)S(1)}, s32[1,2]{1,0:T(1,128)}, u32[]{:S(2)}) copy-start(s32[1,2]{1,0:T(1,128)} %param.12) | copy-start | bytes 28
  14.7 101.9 %all-to-all-start = ((bf16[16,128,2048]{2,1,0:T(8,128)(2,1)}), bf16[16,128,2048]{2,1,0:T(8,128)(2,1)}, u32[]{:S(2)}, u32[]{:S(2)}) async-start(bf16[16,128,2048]{2,1,0:T(8,128)(2,1)} %bitcast.19), calls=%async_computation | async-start | bytes 16777216 | tf_op jit(solution)/shard_map/all_to_all | solution.py:20
  21.3 100.6 %copy-start = (f32[1,128,2048]{2,1,0:T(8,128)S(1)}, f32[1,128,2048]{2,1,0:T(8,128)}, u32[]{:S(2)}) copy-start(f32[1,128,2048]{2,1,0:T(8,128)} %param.7) | copy-start | bytes 3145732
  21.3 100.6 %copy-start.1 = (f32[1,128,2048]{2,1,0:T(8,128)S(1)}, f32[1,128,2048]{2,1,0:T(8,128)}, u32[]{:S(2)}) copy-start(f32[1,128,2048]{2,1,0:T(8,128)} %param.8) | copy-start | bytes 3145732
  121.9 6.5 %copy-start.2 = (f32[8]{0:T(128)S(1)}, f32[8]{0:T(128)}, u32[]{:S(2)}) copy-start(f32[8]{0:T(128)} %param.13) | copy-start | bytes 100
  123.3 16.4 %collective-permute-start.1 = (bf16[1,128,2048]{2,1,0:T(8,128)(2,1)}, bf16[1,128,2048]{2,1,0:T(8,128)(2,1)}, u32[]{:S(2)}, u32[]{:S(2)}) collective-permute-start(bf16[1,128,2048]{2,1,0:T(8,128)(2,1)} %bitcast.6), channel_id=1, source_target_pairs={{0,112},{16,0},{32,16},{48,32},{64,48},{80,64},{96,80},{112,96},{1... | collective-permute-start | bytes 1572872 | tf_op jit(solution)/shard_map/ppermute | solution.py:27
  128.4 17.0 %collective-permute-start = (bf16[1,128,2048]{2,1,0:T(8,128)(2,1)}, bf16[1,128,2048]{2,1,0:T(8,128)(2,1)}, u32[]{:S(2)}, u32[]{:S(2)}) collective-permute-start(bf16[1,128,2048]{2,1,0:T(8,128)(2,1)} %bitcast.6), channel_id=1, source_target_pairs={{0,16},{16,32},{32,48},{48,64},{64,80},{80,96},{96,112},{112,0},{1... | collective-permute-start | bytes 1572872 | tf_op jit(solution)/shard_map/ppermute | solution.py:27
where the time goes:
time: 151 us
  waiting for transfers between devices  110 us (73%)
  matrix products  14 us (9%)
  starting transfers between devices  11.8 us (8%)
  other arithmetic  11.7 us (8%)
  between operations  1.99 us (1%)
    all_to_all x1, waiting for transfers between devices, summed_on_arrival(): blocks = lax.all_to_all(cut_along(value, dim, size), axis, 0, 0, tiled=True)  95.2 us
    ppermute x2, waiting for transfers between devices, shifted(): return lax.ppermute(value, axis, pairs)  15.1 us
    dot_general x1, matrix products, on_device(): lax.dot_general(activations, out_grads, dims, preferred_element_type=jnp....  14 us
    all_to_all x1, starting transfers between devices, summed_on_arrival(): blocks = lax.all_to_all(cut_along(value, dim, size), axis, 0, 0, tiled=True)  6.64 us
    reduce_sum x1, other arithmetic, summed_on_arrival(): return jnp.sum(blocks.astype(jnp.float32), axis=0)  5.3 us
    ppermute x2, starting transfers between devices, shifted(): return lax.ppermute(value, axis, pairs)  5.18 us
    add x1, other arithmetic, on_device(): new_params = stepped + mixing_rate * (new_mixed - new_estimate)  5.1 us
  transfers between devices with their start and end apart: 3, of which 3 were waited for; matrix products, arithmetic and copies ran while one was open for 0% of the time, Pallas kernels for 0%

commit v1 on v0

v1 whole, which is shorter than its diff:
```python
import functools
import math

import jax
import jax.numpy as jnp
from jax import lax
from jax.experimental import pallas as pl
from jax.experimental.pallas import tpu as pltpu
from jax.sharding import PartitionSpec as P

step_size = 0.5
mixing_rate = 0.4

MESH = pl.DeviceIdType.MESH
F32 = jnp.float32
BF16 = jnp.bfloat16
CHUNKS = 8


def aligned(start, size):
    return pl.ds(pl.multiple_of(start, size), size)


def kernel(
    factor,
    params,
    estimate,
    mixed_sum,
    acts,
    grads,
    exponents,
    edge_weight,
    out_p,
    out_e,
    out_m,
    a_v,
    b_v,
    at_v,
    p_v,
    e_v,
    m_v,
    own_v,
    d_src,
    d_dst,
    near_v,
    home_v,
    s1_src,
    s1_dst,
    s2_src,
    s2_dst,
    x_src,
    x_dst,
    g_src,
    g_dst,
    a_sem,
    b_sem,
    l_sem,
    d_sem,
    s1_sem,
    s2_sem,
    x_sem,
    g_sem,
):
    g = lax.axis_index("grp")
    m = lax.axis_index("mem")
    z = m // 4
    x = (m // 2) % 2
    c = m % 2
    pc = 1 - c
    zp, zm, zo = (z + 1) % 4, (z + 3) % 4, (z + 2) % 4
    to_core = (g, z * 4 + x * 2 + pc)
    to_zp = (g, zp * 4 + x * 2 + c)
    to_zm = (g, zm * 4 + x * 2 + c)
    to_x = (g, z * 4 + (1 - x) * 2 + c)
    to_next = ((g + 1) % 8, m)
    to_prev = ((g + 7) % 8, m)
    chunks = CHUNKS
    cw = b_v.shape[2]

    barrier = pltpu.get_barrier_semaphore()
    for peer in (to_core, to_zp, to_zm, to_x, to_next, to_prev):
        pl.semaphore_signal(barrier, inc=1, device_id=peer, device_id_type=MESH)

    def load_a(par, q):
        return pltpu.make_async_copy(
            acts.at[:, aligned((2 * q + par) * 128, 128)], a_v.at[par, q], a_sem.at[par, q]
        )

    def load_b(k):
        return pltpu.make_async_copy(grads.at[:, aligned(k * cw, cw)], b_v.at[k], b_sem.at[k])

    def start_a(par):
        def body(q, _):
            load_a(par, q).start()
            return 0

        lax.fori_loop(0, 8, body, 0)

    start_a(pc)
    load_b(0).start()
    start_a(c)

    def start_b(k, _):
        load_b(k).start()
        return 0

    lax.fori_loop(1, chunks, start_b, 0)
    state = [
        pltpu.make_async_copy(src.at[0], dst, l_sem.at[i])
        for i, (src, dst) in enumerate(((params, p_v), (estimate, e_v), (mixed_sum, m_v)))
    ]
    for copy in state:
        copy.start()

    def transpose_a(par):
        def body(q, _):
            load_a(par, q).wait()
            at_v[par, aligned(q * 128, 128), :] = a_v[par, q].T
            return 0

        lax.fori_loop(0, 8, body, 0)

    def remote(src, dst, sems, index, peer):
        return pltpu.make_async_remote_copy(
            src_ref=src,
            dst_ref=dst,
            send_sem=sems.at[(0,) + index],
            recv_sem=sems.at[(1,) + index],
            device_id=peer,
            device_id_type=MESH,
        )

    def copy_d(k):
        return remote(d_src.at[k], d_dst.at[k], d_sem, (k,), to_core)

    def copy_s1(side, k):
        return remote(
            s1_src.at[side, k], s1_dst.at[side, k], s1_sem, (side, k), (to_zp, to_zm)[side]
        )

    def copy_s2(side, xd, k):
        return remote(
            s2_src.at[side, xd, k],
            s2_dst.at[side, xd, k],
            s2_sem,
            (side, xd, k),
            (to_zp, to_zm)[side],
        )

    def copy_x(k):
        return remote(x_src.at[k], x_dst.at[k], x_sem, (k,), to_x)

    def copy_g(side, k):
        return remote(g_src.at[k], g_dst.at[side, k], g_sem, (side, k), (to_next, to_prev)[side])

    def cols(k):
        return aligned(k * cw, cw)

    def multiply_partner(k):
        d_src[k] = jnp.dot(at_v[pc], b_v[k], preferred_element_type=F32).astype(BF16)
        copy_d(k).start()

    def multiply_own(k):
        own_v[k % 2] = jnp.dot(at_v[c], b_v[k], preferred_element_type=F32)

    def stage_a(k):
        load_b(k).wait()
        multiply_partner(k)
        multiply_own(k)

    def chip_sum(k, zd, xd):
        rows = aligned((zd * 2 + xd) * 128, 128)
        return own_v[k % 2, rows, :] + d_dst[k, rows, :].astype(F32)

    def stage_b(k):
        copy_d(k).wait_recv()
        for side in range(2):
            s1_src[side, k] = chip_sum(k, zo, side).astype(BF16)
            copy_s1(side, k).start()
        for side, zd in enumerate((zp, zm)):
            s2_src[side, 1 - side, k] = chip_sum(k, zd, 1 - side).astype(BF16)
            copy_s2(side, 1 - side, k).start()
        for side, zd in enumerate((zp, zm)):
            near_v[side, k] = chip_sum(k, zd, side)
        for xd in range(2):
            home_v[xd, k] = chip_sum(k, z, xd)

    def stage_c(k):
        for side in range(2):
            copy_s1(side, k).wait_recv()
            s2_src[side, side, k] = (near_v[side, k] + s1_dst[side, k].astype(F32)).astype(BF16)
            copy_s2(side, side, k).start()

    def line_sum(k, xd):
        return home_v[xd, k] + s2_dst[0, xd, k].astype(F32) + s2_dst[1, xd, k].astype(F32)

    def stage_d(k):
        for side in range(2):
            for xd in range(2):
                copy_s2(side, xd, k).wait_recv()
        x_src[k] = line_sum(k, 1 - x).astype(BF16)
        copy_x(k).start()
        home_v[x, k] = line_sum(k, x)

    w_right = edge_weight[g]
    w_left = edge_weight[(g + 7) % 8]
    w_self = 1.0 - w_left - w_right

    def stage_e(k):
        copy_x(k).wait_recv()
        gradient = home_v[x, k] + x_dst[k].astype(F32)
        old = e_v[:, cols(k)]
        stepped = p_v[:, cols(k)] - factor * gradient
        change = stepped - old
        parts = []
        for i in range(2):
            scale = jnp.full((64, cw), lax.shift_left(1, exponents[0, i]).astype(F32), F32)
            levels = jnp.clip(change[i * 64 : (i + 1) * 64] / scale, -1.0, 1.0).astype(BF16)
            parts.append((levels.astype(F32) * scale).astype(BF16))
        compressed = jnp.concatenate(parts, axis=0)
        g_src[k] = compressed
        for side in range(2):
            copy_g(side, k).start()
        piece = compressed.astype(F32)
        out_p[0, :, cols(k)] = stepped
        out_e[0, :, cols(k)] = old + piece
        out_m[0, :, cols(k)] = m_v[:, cols(k)] + w_self * piece

    def stage_f(k):
        for side in range(2):
            copy_g(side, k).wait_recv()
        mixed = out_m[0, :, cols(k)] + w_left * g_dst[0, k].astype(F32)
        mixed = mixed + w_right * g_dst[1, k].astype(F32)
        out_m[0, :, cols(k)] = mixed
        out_p[0, :, cols(k)] = out_p[0, :, cols(k)] + mixing_rate * (mixed - out_e[0, :, cols(k)])

    transpose_a(pc)
    load_b(0).wait()
    pl.semaphore_wait(barrier, 6)
    multiply_partner(0)
    transpose_a(c)
    multiply_own(0)
    for copy in state:
        copy.wait()

    def step(t, _):
        for stage, lag in (
            (stage_a, 0),
            (stage_b, 1),
            (stage_c, 2),
            (stage_d, 3),
            (stage_e, 4),
            (stage_f, 6),
        ):
            pl.when((t >= lag) & (t < chunks + lag))(functools.partial(stage, t - lag))
        return 0

    lax.fori_loop(1, chunks + 6, step, 0)

    def drain(k, _):
        copy_d(k).wait_send()
        copy_x(k).wait_send()
        for side in range(2):
            copy_s1(side, k).wait_send()
            copy_g(side, k).wait_send()
            for xd in range(2):
                copy_s2(side, xd, k).wait_send()
        return 0

    lax.fori_loop(0, chunks, drain, 0)


def on_device(params, estimate, mixed_sum, activations, out_grads, exponents, edge_weight):
    members = lax.axis_size("mem")
    tokens, width = out_grads.shape
    factor = step_size / math.sqrt(members * tokens)
    n = CHUNKS
    cw = width // n
    block = (128, cw)
    shard = jax.ShapeDtypeStruct(params.shape, F32)
    anywhere = pl.BlockSpec(memory_space=pl.ANY)
    vmem = pl.BlockSpec(memory_space=pltpu.VMEM)
    smem = pl.BlockSpec(memory_space=pltpu.SMEM)
    dma = pltpu.SemaphoreType.DMA
    return pl.pallas_call(
        functools.partial(kernel, factor),
        out_shape=(shard, shard, shard),
        in_specs=[anywhere] * 5 + [smem] * 2,
        out_specs=(vmem, vmem, vmem),
        scratch_shapes=[
            pltpu.VMEM((2, 8, tokens, 128), BF16),
            pltpu.VMEM((n, tokens, cw), BF16),
            pltpu.VMEM((2, 1024, tokens), BF16),
            pltpu.VMEM((128, width), F32),
            pltpu.VMEM((128, width), F32),
            pltpu.VMEM((128, width), F32),
            pltpu.VMEM((2, 1024, cw), F32),
            pltpu.VMEM((n, 1024, cw), BF16),
            pltpu.VMEM((n, 1024, cw), BF16),
            pltpu.VMEM((2, n) + block, F32),
            pltpu.VMEM((2, n) + block, F32),
            pltpu.VMEM((2, n) + block, BF16),
            pltpu.VMEM((2, n) + block, BF16),
            pltpu.VMEM((2, 2, n) + block, BF16),
            pltpu.VMEM((2, 2, n) + block, BF16),
            pltpu.VMEM((n,) + block, BF16),
            pltpu.VMEM((n,) + block, BF16),
            pltpu.VMEM((n,) + block, BF16),
            pltpu.VMEM((2, n) + block, BF16),
            dma((2, 8)),
            dma((n,)),
            dma((3,)),
            dma((2, n)),
            dma((2, 2, n)),
            dma((2, 2, 2, n)),
            dma((2, n)),
            dma((2, 2, n)),
        ],
        compiler_params=pltpu.CompilerParams(
            collective_id=0, has_side_effects=True, vmem_limit_bytes=50 * 2**20
        ),
        name="round",
    )(params, estimate, mixed_sum, activations, out_grads, exponents, edge_weight)


def solution(mesh):
    in_specs = (
        P("grp", "mem", None),
        P("grp", "mem", None),
        P("grp", "mem", None),
        P(("grp", "mem"), None),
        P(("grp", "mem"), None),
        P("grp", "mem"),
        P(),
    )
    out_specs = (P("grp", "mem", None), P("grp", "mem", None), P("grp", "mem", None))
    return jax.shard_map(
        on_device, mesh=mesh, in_specs=in_specs, out_specs=out_specs, check_vma=False
    )
```

time: 151 us -> 68.2 us (0.45)
  waiting for transfers between devices: 110 us -> 0 us
  Pallas kernels: 0 us -> 63.2 us
  matrix products: 14 us -> 0 us
  starting transfers between devices: 11.8 us -> 0 us
  other arithmetic: 11.7 us -> 0 us
  local copies, waits for them, and re-layouts: 0.67 us -> 4.21 us
    all_to_all x1 -> x0, waiting for transfers between devices: 95.2 us -> none  [summed_on_arrival(): blocks = lax.all_to_all(cut_along(value, dim, size), axis, 0, 0, tiled=True)]
    pallas_call x0 -> x1, Pallas kernels: none -> 63.2 us  [on_device(): pl.pallas_call(functools.partial(kernel, factor), out_shape=(shard, shard...]
    ppermute x2 -> x0, waiting for transfers between devices: 15.1 us -> none  [shifted(): return lax.ppermute(value, axis, pairs)]
    dot_general x1 -> x0, matrix products: 14 us -> none  [on_device(): lax.dot_general(activations, out_grads, dims, preferred_element_type=jnp....]
    all_to_all x1 -> x0, starting transfers between devices: 6.64 us -> none  [summed_on_arrival(): blocks = lax.all_to_all(cut_along(value, dim, size), axis, 0, 0, tiled=True)]
    reduce_sum x1 -> x0, other arithmetic: 5.3 us -> none  [summed_on_arrival(): return jnp.sum(blocks.astype(jnp.float32), axis=0)]
    ppermute x2 -> x0, starting transfers between devices: 5.18 us -> none  [shifted(): return lax.ppermute(value, axis, pairs)]
    add x1 -> x0, other arithmetic: 5.1 us -> none  [on_device(): new_params = stepped + mixing_rate * (new_mixed - new_estimate)]
  transfers between devices with their start and end apart: 3 -> 0, of which waited for: 3 -> 0; matrix products, arithmetic and copies ran while one was open for 0% -> 0% of each run, Pallas kernels for 0% -> 0%
where the time goes in v1:
time: 68.2 us; the launch traced here: 68.1 us
  Pallas kernels  63.2 us (93%)
  local copies, waits for them, and re-layouts  4.21 us (6%)
    pallas_call x1, Pallas kernels, on_device(): pl.pallas_call(functools.partial(kernel, factor), out_shape=(shard, shard...  63.2 us
    unnamed x7, local copies, waits for them, and re-layouts  4.21 us

profile of v1, /device:TPU:0, one launch (start us, length us, event | category | flops | bytes accessed | tf_op | source)
XLA Modules:
  0.0 68.1 jit_solution(876469276397910092)
XLA Ops:
  0.6 0.0 copy-start
  0.6 0.6 copy-done
  1.3 0.0 copy-start.1
  1.3 0.7 copy-done.1
  1.9 63.2 %round.1 = (f32[1,128,2048]{2,1,0:T(8,128)S(1)}, f32[1,128,2048]{2,1,0:T(8,128)S(1)}, f32[1,128,2048]{2,1,0:T(8,128)S(1)}) custom-call(f32[1,128,2048]{2,1,0:T(8,128)} %params.1, f32[1,128,2048]{2,1,0:T(8,128)} %estimate.1, f32[1,128,2048]{2,1,0:T(8,128)} %mixed_sum.1, bf16[1024,2048]{1,0:T(8,128)(2,1)} %acts.1, bf16[1024,2048]{1,0:T(8,128)(2,1)} %grads.1, ...), custom_call_target="tpu_custom_call" | custom-call | tf_op jit(solution)/shard_map/round/pallas_call | solution.py:285
  65.2 1.0 %copy.13 = f32[1,128,2048]{2,1,0:T(8,128)} copy(f32[1,128,2048]{2,1,0:T(8,128)S(1)} %get-tuple-element.6) | data formatting | bytes 2097152
  66.1 1.0 %copy.14 = f32[1,128,2048]{2,1,0:T(8,128)} copy(f32[1,128,2048]{2,1,0:T(8,128)S(1)} %get-tuple-element.7) | data formatting | bytes 2097152
  67.1 1.0 %copy.15 = f32[1,128,2048]{2,1,0:T(8,128)} copy(f32[1,128,2048]{2,1,0:T(8,128)S(1)} %get-tuple-element.8) | data formatting | bytes 2097152
Async XLA Ops:
  0.6 0.7 copy-start
  1.3 0.7 copy-start.1

commit v2 on v1

v2 whole, which is shorter than its diff:
```python
import functools
import math

import jax
import jax.numpy as jnp
from jax import lax
from jax.experimental import pallas as pl
from jax.experimental.pallas import tpu as pltpu
from jax.sharding import PartitionSpec as P

step_size = 0.5
mixing_rate = 0.4

MESH = pl.DeviceIdType.MESH
F32 = jnp.float32
BF16 = jnp.bfloat16
CHUNKS = 8
WIDE = 2
HEAD = 2


def aligned(start, size):
    return pl.ds(pl.multiple_of(start, size), size)


def kernel(
    factor,
    params,
    estimate,
    mixed_sum,
    acts,
    grads,
    exponents,
    edge_weight,
    out_p,
    out_e,
    out_m,
    a_v,
    b_v,
    at_v,
    p_v,
    e_v,
    m_v,
    own_v,
    d_src,
    d_dst,
    near_v,
    home_v,
    s1_src,
    s1_dst,
    s2_src,
    s2_dst,
    x_src,
    x_dst,
    wide_own,
    wide_src,
    wide_dst,
    near_w,
    home_w,
    w1_src,
    w1_dst,
    w2_src,
    w2_dst,
    g_src,
    g_dst,
    h_src,
    h_dst,
    powers,
    weights,
    a_sem,
    b_sem,
    l_sem,
    d_sem,
    head_sem,
    s1_sem,
    s2_sem,
    x_sem,
    wide_sem,
    w1_sem,
    w2_sem,
    g_sem,
    h_sem,
):
    g = lax.axis_index("grp")
    m = lax.axis_index("mem")
    z = m // 4
    x = (m // 2) % 2
    c = m % 2
    pc = 1 - c
    zp, zm, zo = (z + 1) % 4, (z + 3) % 4, (z + 2) % 4
    to_core = (g, z * 4 + x * 2 + pc)
    to_line = ((g, zp * 4 + x * 2 + c), (g, zm * 4 + x * 2 + c))
    to_x = (g, z * 4 + (1 - x) * 2 + c)
    to_cycle = (((g + 1) % 8, m), ((g + 7) % 8, m))
    chunks, _, cw = b_v.shape
    pieces, _, _, pw = wide_src.shape
    wide = pieces * pw // cw
    slim = chunks - wide
    line = (zo, zp, zm, z)

    barrier = pltpu.get_barrier_semaphore()
    for peer in (to_core, to_x) + to_line + to_cycle:
        pl.semaphore_signal(barrier, inc=1, device_id=peer, device_id_type=MESH)

    def load_a(i, slot):
        j, xd, par = i
        block = line[j] * 4 + xd * 2 + (pc, c)[par]
        return pltpu.make_async_copy(
            acts.at[:, aligned(block * 128, 128)], a_v.at[slot], a_sem.at[slot]
        )

    def load_b(k):
        return pltpu.make_async_copy(grads.at[:, aligned(k * cw, cw)], b_v.at[k], b_sem.at[k])

    blocks = [(0, xd, par) for par in range(2) for xd in range(2)]
    blocks += [(j, xd, par) for par in range(2) for j in range(1, 4) for xd in range(2)]
    for slot, i in enumerate(blocks):
        if slot == 4:
            for k in range(HEAD):
                load_b(k).start()
        load_a(i, slot).start()
    small = [
        pltpu.make_async_copy(exponents, powers, l_sem.at[3]),
        pltpu.make_async_copy(edge_weight, weights, l_sem.at[4]),
    ]
    state = [
        pltpu.make_async_copy(src.at[0], dst, l_sem.at[i])
        for i, (src, dst) in enumerate(((params, p_v), (estimate, e_v), (mixed_sum, m_v)))
    ]
    for k in (slim, HEAD, *range(slim + 1, chunks), *range(HEAD + 1, slim)):
        load_b(k).start()
    for copy in small + state:
        copy.start()

    def transpose_a(low, high):
        def body(slot, _):
            pltpu.make_async_copy(
                acts.at[:, pl.ds(0, 128)], a_v.at[slot], a_sem.at[slot]
            ).wait()
            at_v[aligned(slot * 128, 128), :] = a_v[slot].T
            return 0

        lax.fori_loop(low, high, body, 0)

    def remote(src, dst, sems, index, peer):
        return pltpu.make_async_remote_copy(
            src_ref=src,
            dst_ref=dst,
            send_sem=sems.at[(0,) + index],
            recv_sem=sems.at[(1,) + index],
            device_id=peer,
            device_id_type=MESH,
        )

    def copy_d(k):
        return remote(d_src.at[k], d_dst.at[k], d_sem, (k,), to_core)

    def copy_head(k):
        rows = pl.ds(0, 256)
        return remote(d_src.at[k, rows], d_dst.at[k, rows], head_sem, (k,), to_core)

    def copy_rest(k):
        rows = pl.ds(256, 768)
        return remote(d_src.at[k, rows], d_dst.at[k, rows], d_sem, (k,), to_core)

    def copy_s1(side, k):
        return remote(
            s1_src.at[side, k], s1_dst.at[side, k], s1_sem, (side, k), to_line[side]
        )

    def copy_s2(side, xd, k):
        return remote(
            s2_src.at[side, xd, k],
            s2_dst.at[side, xd, k],
            s2_sem,
            (side, xd, k),
            to_line[side],
        )

    def copy_x(k):
        return remote(x_src.at[k], x_dst.at[k], x_sem, (k,), to_x)

    def copy_wide(i):
        return remote(wide_src.at[i], wide_dst.at[i], wide_sem, (i,), to_x)

    def copy_w1(side, i):
        return remote(
            w1_src.at[side, i], w1_dst.at[side, i], w1_sem, (side, i), to_line[side]
        )

    def copy_w2(side, half, i):
        return remote(
            w2_src.at[side, half, i],
            w2_dst.at[side, half, i],
            w2_sem,
            (side, half, i),
            to_line[side],
        )

    def copy_g(side, k):
        return remote(
            g_src.at[k], g_dst.at[side, k], g_sem, (side, k), to_cycle[side]
        )

    def copy_h(side, i):
        return remote(
            h_src.at[i], h_dst.at[side, i], h_sem, (side, i), to_cycle[side]
        )

    def multiply(k, slot):
        load_b(k).wait()
        both = jnp.dot(at_v[...], b_v[k], preferred_element_type=F32)
        d_src[k, pl.ds(0, 256), :] = both[:256].astype(BF16)
        own_v[slot, pl.ds(0, 256), :] = both[256:512]
        d_src[k, pl.ds(256, 768), :] = both[512:1280].astype(BF16)
        own_v[slot, pl.ds(256, 768), :] = both[1280:]
        copy_d(k).start()

    def multiply_head(k, _):
        load_b(k).wait()
        both = jnp.dot(at_v[pl.ds(0, 512), :], b_v[k], preferred_element_type=F32)
        d_src[k, pl.ds(0, 256), :] = both[:256].astype(BF16)
        own_v[k, pl.ds(0, 256), :] = both[256:]
        return 0

    def multiply_rest(k, _):
        both = jnp.dot(at_v[pl.ds(512, 1536), :], b_v[k], preferred_element_type=F32)
        d_src[k, pl.ds(256, 768), :] = both[:768].astype(BF16)
        own_v[k, pl.ds(256, 768), :] = both[768:]
        copy_rest(k).start()
        return 0

    def slim_multiply(k):
        multiply(k, k % 2)

    def wide_multiply(i):
        multiply(slim + i, 2 + i)

    def chip_sum(k, slot, j, xd):
        rows = aligned((j * 2 + xd) * 128, 128)
        return own_v[slot, rows, :] + d_dst[k, rows, :].astype(F32)

    def send_first(k):
        for side in range(2):
            s1_src[side, k] = chip_sum(k, k % 2, 0, side).astype(BF16)
            copy_s1(side, k).start()

    def send_direct(k):
        part = functools.partial(chip_sum, k, k % 2)
        for side in range(2):
            s2_src[side, 1 - side, k] = part(1 + side, 1 - side).astype(BF16)
            copy_s2(side, 1 - side, k).start()
        for side in range(2):
            near_v[side, k] = part(1 + side, side)
        for xd in range(2):
            home_v[xd, k] = part(3, xd)

    def head_first(k):
        copy_head(k).wait_recv()
        send_first(k)

    def head_direct(k):
        copy_rest(k).wait_recv()
        send_direct(k)

    def slim_first(k):
        k = k + HEAD
        copy_d(k).wait_recv()
        send_first(k)
        send_direct(k)

    def slim_relay(k):
        for side in range(2):
            copy_s1(side, k).wait_recv()
            s2_src[side, side, k] = (near_v[side, k] + s1_dst[side, k].astype(F32)).astype(BF16)
            copy_s2(side, side, k).start()

    def slim_cross(k):
        for side in range(2):
            for xd in range(2):
                copy_s2(side, xd, k).wait_recv()

        def line_sum(xd):
            return home_v[xd, k] + s2_dst[0, xd, k].astype(F32) + s2_dst[1, xd, k].astype(F32)

        x_src[k] = line_sum(1 - x).astype(BF16)
        copy_x(k).start()
        home_v[x, k] = line_sum(x)

    def slim_finish(k):
        copy_x(k).wait_recv()
        compress(aligned(k * cw, cw), home_v[x, k] + x_dst[k].astype(F32), g_src.at[k])
        for side in range(2):
            copy_g(side, k).start()

    def wide_first(i):
        k = slim + i
        copy_d(k).wait_recv()
        for j in range(4):
            away = chip_sum(k, 2 + i, j, 1 - x).astype(BF16)
            for part in range(cw // pw):
                wide_src[i * (cw // pw) + part, j] = away[:, part * pw : (part + 1) * pw]
        for part in range(cw // pw):
            copy_wide(i * (cw // pw) + part).start()
        for j in range(4):
            keep = chip_sum(k, 2 + i, j, x)
            for part in range(cw // pw):
                wide_own[i * (cw // pw) + part, j] = keep[:, part * pw : (part + 1) * pw]

    def wide_line(i):
        copy_wide(i).wait_recv()

        def pair_sum(j, half):
            rows = pl.ds(half * 64, 64)
            return wide_own[i, j, rows, :] + wide_dst[i, j, rows, :].astype(F32)

        for side in range(2):
            w1_src[side, i] = pair_sum(0, side).astype(BF16)
            copy_w1(side, i).start()
        for side in range(2):
            w2_src[side, 1 - side, i] = pair_sum(1 + side, 1 - side).astype(BF16)
            copy_w2(side, 1 - side, i).start()
        for side in range(2):
            near_w[side, i] = pair_sum(1 + side, side)
        for half in range(2):
            home_w[half, i] = pair_sum(3, half)

    def wide_relay(i):
        for side in range(2):
            copy_w1(side, i).wait_recv()
            w2_src[side, side, i] = (near_w[side, i] + w1_dst[side, i].astype(F32)).astype(BF16)
            copy_w2(side, side, i).start()

    def wide_finish(i):
        for side in range(2):
            for half in range(2):
                copy_w2(side, half, i).wait_recv()
        sums = [
            home_w[half, i] + w2_dst[0, half, i].astype(F32) + w2_dst[1, half, i].astype(F32)
            for half in range(2)
        ]
        start = slim * cw + i * pw
        compress(aligned(start, pw), jnp.concatenate(sums, axis=0), h_src.at[i])
        for side in range(2):
            copy_h(side, i).start()

    for copy in small:
        copy.wait()
    w_right = weights[g]
    w_left = weights[(g + 7) % 8]
    w_self = 1.0 - w_left - w_right

    def compress(cols, gradient, sent):
        old = e_v[:, cols]
        stepped = p_v[:, cols] - factor * gradient
        change = stepped - old
        parts = []
        for i in range(2):
            scale = lax.shift_left(1, powers[0, i]).astype(F32)
            scale = jnp.full((64, change.shape[1]), scale, F32)
            levels = jnp.clip(change[i * 64 : (i + 1) * 64] / scale, -1.0, 1.0).astype(BF16)
            parts.append((levels.astype(F32) * scale).astype(BF16))
        compressed = jnp.concatenate(parts, axis=0)
        sent[...] = compressed
        piece = compressed.astype(F32)
        out_p[0, :, cols] = stepped
        out_e[0, :, cols] = old + piece
        out_m[0, :, cols] = m_v[:, cols] + w_self * piece

    def mix(cols, left, right):
        mixed = out_m[0, :, cols] + w_left * left[...].astype(F32)
        mixed = mixed + w_right * right[...].astype(F32)
        out_m[0, :, cols] = mixed
        out_p[0, :, cols] = out_p[0, :, cols] + mixing_rate * (mixed - out_e[0, :, cols])

    def slim_mix(k):
        for side in range(2):
            copy_g(side, k).wait_recv()
        mix(aligned(k * cw, cw), g_dst.at[0, k], g_dst.at[1, k])

    def wide_mix(i):
        for side in range(2):
            copy_h(side, i).wait_recv()
        mix(aligned(slim * cw + i * pw, pw), h_dst.at[0, i], h_dst.at[1, i])

    transpose_a(0, 4)
    lax.fori_loop(0, HEAD, multiply_head, 0)
    pl.semaphore_wait(barrier, 6)
    for k in range(HEAD):
        copy_head(k).start()
    transpose_a(4, 16)
    for k in range(HEAD):
        head_first(k)
    lax.fori_loop(0, HEAD, multiply_rest, 0)
    for copy in state:
        copy.wait()

    def step(t, _):
        for stage, lag, count in (
            (head_direct, 0, HEAD),
            (slim_first, HEAD, slim - HEAD),
            (wide_line, 4, pieces),
            (slim_relay, 1, slim),
            (wide_relay, 6, pieces),
            (lambda i: slim_multiply(i + HEAD), 1, slim - HEAD),
            (wide_multiply, 0, wide),
            (wide_first, 1, wide),
            (slim_cross, 3, slim),
            (wide_finish, 8, pieces),
            (slim_finish, 4, slim),
            (slim_mix, 7, slim),
            (wide_mix, 11, pieces),
        ):
            pl.when((t >= lag) & (t < count + lag))(functools.partial(stage, t - lag))
        return 0

    lax.fori_loop(0, 15, step, 0)

    def drain_slim(k, _):
        copy_x(k).wait_send()
        for side in range(2):
            copy_g(side, k).wait_send()
            copy_s1(side, k).wait_send()
            for xd in range(2):
                copy_s2(side, xd, k).wait_send()
        return 0

    def drain_wide(i, _):
        copy_wide(i).wait_send()
        for side in range(2):
            copy_h(side, i).wait_send()
            copy_w1(side, i).wait_send()
            for half in range(2):
                copy_w2(side, half, i).wait_send()
        return 0

    def drain_head(k, _):
        copy_head(k).wait_send()
        copy_rest(k).wait_send()
        return 0

    def drain(k, _):
        copy_d(k).wait_send()
        return 0

    lax.fori_loop(0, slim, drain_slim, 0)
    lax.fori_loop(0, pieces, drain_wide, 0)
    lax.fori_loop(0, HEAD, drain_head, 0)
    lax.fori_loop(HEAD, chunks, drain, 0)


def store(in_p, in_e, in_m, out_p, out_e, out_m, sems):
    copies = [
        pltpu.make_async_copy(src, dst, sems.at[i])
        for i, (src, dst) in enumerate(((in_p, out_p), (in_e, out_e), (in_m, out_m)))
    ]
    for copy in copies:
        copy.start()
    for copy in copies:
        copy.wait()


def on_device(params, estimate, mixed_sum, activations, out_grads, exponents, edge_weight):
    members = lax.axis_size("mem")
    tokens, width = out_grads.shape
    factor = step_size / math.sqrt(members * tokens)
    n = CHUNKS
    cw = width // n
    w = WIDE
    r = n - w
    p = w * cw // 128
    block = (128, cw)
    piece = (128, 128)
    half = (64, 128)
    shard = jax.ShapeDtypeStruct(params.shape, F32)
    anywhere = pl.BlockSpec(memory_space=pl.ANY)
    hbm = pl.BlockSpec(memory_space=pltpu.HBM)
    vmem = pl.BlockSpec(memory_space=pltpu.VMEM)
    dma = pltpu.SemaphoreType.DMA
    exponents = pltpu.with_memory_space_constraint(exponents, pltpu.HBM)
    edge_weight = pltpu.with_memory_space_constraint(edge_weight, pltpu.HBM)
    results = pl.pallas_call(
        functools.partial(kernel, factor),
        out_shape=(shard, shard, shard),
        in_specs=[hbm] * 7,
        out_specs=(vmem, vmem, vmem),
        scratch_shapes=[
            pltpu.VMEM((16, tokens, 128), BF16),
            pltpu.VMEM((n, tokens, cw), BF16),
            pltpu.VMEM((2048, tokens), BF16),
            pltpu.VMEM((128, width), F32),
            pltpu.VMEM((128, width), F32),
            pltpu.VMEM((128, width), F32),
            pltpu.VMEM((2 + w, 1024, cw), F32),
            pltpu.VMEM((n, 1024, cw), BF16),
            pltpu.VMEM((n, 1024, cw), BF16),
            pltpu.VMEM((2, r) + block, F32),
            pltpu.VMEM((2, r) + block, F32),
            pltpu.VMEM((2, r) + block, BF16),
            pltpu.VMEM((2, r) + block, BF16),
            pltpu.VMEM((2, 2, r) + block, BF16),
            pltpu.VMEM((2, 2, r) + block, BF16),
            pltpu.VMEM((r,) + block, BF16),
            pltpu.VMEM((r,) + block, BF16),
            pltpu.VMEM((p, 4) + piece, F32),
            pltpu.VMEM((p, 4) + piece, BF16),
            pltpu.VMEM((p, 4) + piece, BF16),
            pltpu.VMEM((2, p) + half, F32),
            pltpu.VMEM((2, p) + half, F32),
            pltpu.VMEM((2, p) + half, BF16),
            pltpu.VMEM((2, p) + half, BF16),
            pltpu.VMEM((2, 2, p) + half, BF16),
            pltpu.VMEM((2, 2, p) + half, BF16),
            pltpu.VMEM((r,) + block, BF16),
            pltpu.VMEM((2, r) + block, BF16),
            pltpu.VMEM((p,) + piece, BF16),
            pltpu.VMEM((2, p) + piece, BF16),
            pltpu.SMEM((1, 2), jnp.int32),
            pltpu.SMEM((8,), F32),
            dma((16,)),
            dma((n,)),
            dma((5,)),
            dma((2, n)),
            dma((2, HEAD)),
            dma((2, 2, r)),
            dma((2, 2, 2, r)),
            dma((2, r)),
            dma((2, p)),
            dma((2, 2, p)),
            dma((2, 2, 2, p)),
            dma((2, 2, r)),
            dma((2, 2, p)),
        ],
        compiler_params=pltpu.CompilerParams(
            collective_id=0, has_side_effects=True, vmem_limit_bytes=50 * 2**20
        ),
        name="round",
    )(params, estimate, mixed_sum, activations, out_grads, exponents, edge_weight)
    return pl.pallas_call(
        store,
        out_shape=(shard, shard, shard),
        in_specs=[vmem] * 3,
        out_specs=(anywhere,) * 3,
        scratch_shapes=[dma((3,))],
        compiler_params=pltpu.CompilerParams(vmem_limit_bytes=2**20),
        name="store",
    )(*results)


def solution(mesh):
    in_specs = (
        P("grp", "mem", None),
        P("grp", "mem", None),
        P("grp", "mem", None),
        P(("grp", "mem"), None),
        P(("grp", "mem"), None),
        P("grp", "mem"),
        P(),
    )
    out_specs = (P("grp", "mem", None), P("grp", "mem", None), P("grp", "mem", None))
    return jax.shard_map(
        on_device, mesh=mesh, in_specs=in_specs, out_specs=out_specs, check_vma=False
    )
```

time: 68.2 us -> 56.5 us (0.83)
  Pallas kernels: 63.2 us -> 55.8 us
  local copies, waits for them, and re-layouts: 4.21 us -> 0 us
    pallas_call x1, Pallas kernels: 63.2 us -> 54.1 us  [on_device(): pl.pallas_call(functools.partial(kernel, factor), out_shape=(shard, shard...]
    unnamed x7 -> x0, local copies, waits for them, and re-layouts: 4.21 us -> none
    pallas_call x0 -> x1, Pallas kernels: none -> 1.69 us  [on_device(): pl.pallas_call(store, out_shape=(shard, shard, shard), in_specs=[vmem] *...]
where the time goes in v2:
time: 56.5 us; the launch traced here: 56.4 us
  Pallas kernels  55.8 us (99%)
  between operations  0.64 us (1%)
    pallas_call x1, Pallas kernels, on_device(): pl.pallas_call(functools.partial(kernel, factor), out_shape=(shard, shard...  54.1 us
    pallas_call x1, Pallas kernels, on_device(): pl.pallas_call(store, out_shape=(shard, shard, shard), in_specs=[vmem] *...  1.69 us

profile of v2, /device:TPU:0, one launch (start us, length us, event | category | flops | bytes accessed | tf_op | source)
XLA Modules:
  0.0 56.4 jit_solution(15816288902449142646)
XLA Ops:
  0.6 54.1 %round.1 = (f32[1,128,2048]{2,1,0:T(8,128)S(1)}, f32[1,128,2048]{2,1,0:T(8,128)S(1)}, f32[1,128,2048]{2,1,0:T(8,128)S(1)}) custom-call(f32[1,128,2048]{2,1,0:T(8,128)} %params.1, f32[1,128,2048]{2,1,0:T(8,128)} %estimate.1, f32[1,128,2048]{2,1,0:T(8,128)} %mixed_sum.1, bf16[1024,2048]{1,0:T(8,128)(2,1)} %acts.1, bf16[1024,2048]{1,0:T(8,128)(2,1)} %grads.1, ...), custom_call_target="tpu_custom_call" | custom-call | tf_op jit(solution)/shard_map/round/pallas_call | solution.py:482
  54.7 1.7 %store.1 = (f32[1,128,2048]{2,1,0:T(8,128)}, f32[1,128,2048]{2,1,0:T(8,128)}, f32[1,128,2048]{2,1,0:T(8,128)}) custom-call(f32[1,128,2048]{2,1,0:T(8,128)S(1)} %get-tuple-element.6.in_p, f32[1,128,2048]{2,1,0:T(8,128)S(1)} %get-tuple-element.7.in_e, f32[1,128,2048]{2,1,0:T(8,128)S(1)} %get-tuple-element.8.in_m), custom_call_target="tpu_custom_call" | custom-call | tf_op jit(solution)/shard_map/store/pallas_call | solution.py:539

commit v3 on v2

--- a/solution.py
+++ b/solution.py
@@ -395,19 +395,51 @@
     for copy in state:
         copy.wait()
 
+    def drain_slim(k, _):
+        copy_x(k).wait_send()
+        for side in range(2):
+            copy_s1(side, k).wait_send()
+            for xd in range(2):
+                copy_s2(side, xd, k).wait_send()
+        return 0
+
+    def drain_wide(i, _):
+        copy_wide(i).wait_send()
+        for side in range(2):
+            copy_w1(side, i).wait_send()
+            for half in range(2):
+                copy_w2(side, half, i).wait_send()
+        return 0
+
+    def drain_head(k, _):
+        copy_head(k).wait_send()
+        copy_rest(k).wait_send()
+        return 0
+
+    def drain(k, _):
+        copy_d(k).wait_send()
+        return 0
+
+    def drain_early():
+        lax.fori_loop(0, slim, drain_slim, 0)
+        lax.fori_loop(0, pieces, drain_wide, 0)
+        lax.fori_loop(0, HEAD, drain_head, 0)
+        lax.fori_loop(HEAD, chunks, drain, 0)
+
     def step(t, _):
         for stage, lag, count in (
             (head_direct, 0, HEAD),
             (slim_first, HEAD, slim - HEAD),
-            (wide_line, 4, pieces),
             (slim_relay, 1, slim),
-            (wide_relay, 6, pieces),
             (lambda i: slim_multiply(i + HEAD), 1, slim - HEAD),
             (wide_multiply, 0, wide),
             (wide_first, 1, wide),
+            (wide_line, 4, pieces),
+            (wide_relay, 6, pieces),
             (slim_cross, 3, slim),
             (wide_finish, 8, pieces),
             (slim_finish, 4, slim),
+            (lambda i: drain_early(), pieces + 8, 1),
             (slim_mix, 7, slim),
             (wide_mix, 11, pieces),
         ):
@@ -416,37 +448,18 @@
 
     lax.fori_loop(0, 15, step, 0)
 
-    def drain_slim(k, _):
-        copy_x(k).wait_send()
+    def drain_slim_cycle(k, _):
         for side in range(2):
             copy_g(side, k).wait_send()
-            copy_s1(side, k).wait_send()
-            for xd in range(2):
-                copy_s2(side, xd, k).wait_send()
-        return 0
-
-    def drain_wide(i, _):
-        copy_wide(i).wait_send()
+        return 0
+
+    def drain_wide_cycle(i, _):
         for side in range(2):
             copy_h(side, i).wait_send()
-            copy_w1(side, i).wait_send()
-            for half in range(2):
-                copy_w2(side, half, i).wait_send()
-        return 0
-
-    def drain_head(k, _):
-        copy_head(k).wait_send()
-        copy_rest(k).wait_send()
-        return 0
-
-    def drain(k, _):
-        copy_d(k).wait_send()
-        return 0
-
-    lax.fori_loop(0, slim, drain_slim, 0)
-    lax.fori_loop(0, pieces, drain_wide, 0)
-    lax.fori_loop(0, HEAD, drain_head, 0)
-    lax.fori_loop(HEAD, chunks, drain, 0)
+        return 0
+
+    lax.fori_loop(0, slim, drain_slim_cycle, 0)
+    lax.fori_loop(0, pieces, drain_wide_cycle, 0)
 
 
 def store(in_p, in_e, in_m, out_p, out_e, out_m, sems):

time: 56.5 us -> 56.2 us (level)
  no operation moved by 1% of the time
where the time goes in v3:
time: 56.2 us; the launch traced here: 56.1 us
  Pallas kernels  55.4 us (99%)
  between operations  0.64 us (1%)
    pallas_call x1, Pallas kernels, on_device(): pl.pallas_call(functools.partial(kernel, factor), out_shape=(shard, shard...  53.7 us
    pallas_call x1, Pallas kernels, on_device(): pl.pallas_call(store, out_shape=(shard, shard, shard), in_specs=[vmem] *...  1.69 us

profile of v3, /device:TPU:0, one launch (start us, length us, event | category | flops | bytes accessed | tf_op | source)
XLA Modules:
  0.0 56.1 jit_solution(10449214093923731295)
XLA Ops:
  0.6 53.7 %round.1 = (f32[1,128,2048]{2,1,0:T(8,128)S(1)}, f32[1,128,2048]{2,1,0:T(8,128)S(1)}, f32[1,128,2048]{2,1,0:T(8,128)S(1)}) custom-call(f32[1,128,2048]{2,1,0:T(8,128)} %params.1, f32[1,128,2048]{2,1,0:T(8,128)} %estimate.1, f32[1,128,2048]{2,1,0:T(8,128)} %mixed_sum.1, bf16[1024,2048]{1,0:T(8,128)(2,1)} %acts.1, bf16[1024,2048]{1,0:T(8,128)(2,1)} %grads.1, ...), custom_call_target="tpu_custom_call" | custom-call | tf_op jit(solution)/shard_map/round/pallas_call | solution.py:495
  54.4 1.7 %store.1 = (f32[1,128,2048]{2,1,0:T(8,128)}, f32[1,128,2048]{2,1,0:T(8,128)}, f32[1,128,2048]{2,1,0:T(8,128)}) custom-call(f32[1,128,2048]{2,1,0:T(8,128)S(1)} %get-tuple-element.6.in_p, f32[1,128,2048]{2,1,0:T(8,128)S(1)} %get-tuple-element.7.in_e, f32[1,128,2048]{2,1,0:T(8,128)S(1)} %get-tuple-element.8.in_m), custom_call_target="tpu_custom_call" | custom-call | tf_op jit(solution)/shard_map/store/pallas_call | solution.py:552

commit v4 on v3

--- a/solution.py
+++ b/solution.py
@@ -432,11 +432,11 @@
             (slim_first, HEAD, slim - HEAD),
             (slim_relay, 1, slim),
             (lambda i: slim_multiply(i + HEAD), 1, slim - HEAD),
+            (slim_cross, 3, slim),
             (wide_multiply, 0, wide),
             (wide_first, 1, wide),
             (wide_line, 4, pieces),
             (wide_relay, 6, pieces),
-            (slim_cross, 3, slim),
             (wide_finish, 8, pieces),
             (slim_finish, 4, slim),
             (lambda i: drain_early(), pieces + 8, 1),

time: 56.2 us -> 56.1 us (level)
  no operation moved by 1% of the time
where the time goes in v4:
time: 56.1 us; the launch traced here: 56 us
  Pallas kernels  55.4 us (99%)
  between operations  0.64 us (1%)
    pallas_call x1, Pallas kernels, on_device(): pl.pallas_call(functools.partial(kernel, factor), out_shape=(shard, shard...  53.7 us
    pallas_call x1, Pallas kernels, on_device(): pl.pallas_call(store, out_shape=(shard, shard, shard), in_specs=[vmem] *...  1.69 us

profile of v4, /device:TPU:0, one launch (start us, length us, event | category | flops | bytes accessed | tf_op | source)
XLA Modules:
  0.0 56.0 jit_solution(15651445242800996150)
XLA Ops:
  0.6 53.7 %round.1 = (f32[1,128,2048]{2,1,0:T(8,128)S(1)}, f32[1,128,2048]{2,1,0:T(8,128)S(1)}, f32[1,128,2048]{2,1,0:T(8,128)S(1)}) custom-call(f32[1,128,2048]{2,1,0:T(8,128)} %params.1, f32[1,128,2048]{2,1,0:T(8,128)} %estimate.1, f32[1,128,2048]{2,1,0:T(8,128)} %mixed_sum.1, bf16[1024,2048]{1,0:T(8,128)(2,1)} %acts.1, bf16[1024,2048]{1,0:T(8,128)(2,1)} %grads.1, ...), custom_call_target="tpu_custom_call" | custom-call | tf_op jit(solution)/shard_map/round/pallas_call | solution.py:495
  54.3 1.7 %store.1 = (f32[1,128,2048]{2,1,0:T(8,128)}, f32[1,128,2048]{2,1,0:T(8,128)}, f32[1,128,2048]{2,1,0:T(8,128)}) custom-call(f32[1,128,2048]{2,1,0:T(8,128)S(1)} %get-tuple-element.6.in_p, f32[1,128,2048]{2,1,0:T(8,128)S(1)} %get-tuple-element.7.in_e, f32[1,128,2048]{2,1,0:T(8,128)S(1)} %get-tuple-element.8.in_m), custom_call_target="tpu_custom_call" | custom-call | tf_op jit(solution)/shard_map/store/pallas_call | solution.py:552
